TPU v7x, 32 devices: a whole 2x2x4 slice. The times are simulated.
32 devices in a mesh: ctx: 8 (over z, x), head: 4 (over y, core).
Axes of the slice: x: 2, y: 2, z: 4, core: 2. Of those that a mesh axis runs over, the one named last changes fastest.
Arguments:
- query: bfloat16 [6144, 1024], P('ctx', 'head'), parts along dimension 1, may hold values from -6 to 6
- key_value: bfloat16 [6144, 1024], P('ctx', 'head'), parts along dimension 1, may hold values from -6 to 6
- d_out: bfloat16 [6144, 1024], P('ctx', 'head'), parts along dimension 1, may hold values from -128 to 128
- doc_starts: int32 [64], P('head'), parts along dimension 0, may hold values from 0 to 6143, as said below
Outputs:
- d_query: bfloat16 [6144, 1024], P('ctx', 'head'), parts along dimension 1
- d_key_value: bfloat16 [6144, 1024], P('ctx', 'head'), parts along dimension 1
There are 4 independent parts, one for each index of `head`. A program takes and returns all parts, laid end to end along the dimension named above; each array names one. Nothing has to cross between parts.
Inputs may be any that keep to these rules, and one draw needn't show every extreme that they name: `doc_starts`: Non-decreasing, first entry 0; the document of position p runs from the largest entry not above p up to the next larger entry or 6144; repeated entries are empty documents. A position p never belongs to a document that begins before (p // 768 - 3) * 768, and in every draw some document begins in the block of 768 positions exactly 3 blocks before the block of its last position.
All inputs are finite; a program needn't handle non-finite values.
Results may differ from a plain program's by a relative error of at most 0.0055.
Values may be sent and summed in bfloat16 or wider, within the bound.
A program may use at most 128 MiB of HBM per device.

v0:
```python
import jax
import jax.numpy as jnp
from jax import lax
from jax.sharding import PartitionSpec as P

HOPS = 3


def shifted(value, axis, steps):
    count = lax.axis_size(axis)
    first, last = (max(0, -steps), min(count, count - steps))
    return lax.ppermute(value, axis, [(source, source + steps) for source in range(first, last)])


def shards(query, key_value, d_out, doc_starts):
    tok_rows = query.shape[0]
    head_width = key_value.shape[1] // 2
    head_count = query.shape[1] // head_width
    score_scale = head_width ** (-0.5)
    shard_index = lax.axis_index("ctx")
    positions = shard_index * tok_rows + jnp.arange(tok_rows, dtype=jnp.int32)
    earlier = doc_starts[None, :] <= positions[:, None]
    owners = jnp.max(jnp.where(earlier, doc_starts[None, :], 0), axis=1)
    queries = query.reshape(tok_rows, head_count, head_width)
    grads_out = d_out.reshape(tok_rows, head_count, head_width)
    fetched = [key_value]
    for offset in range(1, HOPS + 1):
        fetched.append(shifted(key_value, "ctx", offset))

    def key_root(offset):
        return (shard_index - offset) * tok_rows

    def visible_pairs(offset):
        key_pos = key_root(offset) + jnp.arange(tok_rows, dtype=jnp.int32)
        return ((key_pos[None, :] >= owners[:, None]) & (key_pos[None, :] <= positions[:, None]))[
            None
        ]

    def scores_of(kv_block):
        return (
            jnp.einsum(
                "thd,sd->hts", queries, kv_block[:, :head_width], preferred_element_type=jnp.float32
            )
            * score_scale
        )

    def grad_prob_of(kv_block):
        return jnp.einsum(
            "thd,sd->hts", grads_out, kv_block[:, head_width:], preferred_element_type=jnp.float32
        )

    running = (
        jnp.full((head_count, tok_rows), -jnp.inf, jnp.float32),
        jnp.zeros((head_count, tok_rows), jnp.float32),
        jnp.zeros((head_count, tok_rows), jnp.float32),
    )
    for offset in range(HOPS + 1):
        absorb_kv_block = fetched[offset]
        absorb_row_top, absorb_row_total, absorb_weighted = running
        absorb_visible = visible_pairs(offset)
        absorb_scores = scores_of(absorb_kv_block)
        absorb_grad_prob = grad_prob_of(absorb_kv_block)
        block_top = jnp.max(jnp.where(absorb_visible, absorb_scores, -jnp.inf), axis=2)
        new_top = jnp.maximum(absorb_row_top, block_top)
        factor = jnp.exp(absorb_row_top - new_top)
        expos = jnp.where(absorb_visible, jnp.exp(absorb_scores - new_top[:, :, None]), 0.0)
        running = (
            new_top,
            absorb_row_total * factor + jnp.sum(expos, axis=2),
            absorb_weighted * factor + jnp.sum(expos * absorb_grad_prob, axis=2),
        )
    row_top, row_total, weighted = running
    log_total = row_top + jnp.log(row_total)
    row_delta = weighted / row_total
    query_grads = jnp.zeros((tok_rows, head_count, head_width), jnp.float32)
    shares = []
    for offset in range(HOPS + 1):
        gradients_kv_block = fetched[offset]
        visible = visible_pairs(offset)
        scores = scores_of(gradients_kv_block)
        weights = jnp.where(visible, jnp.exp(scores - log_total[:, :, None]), 0.0)
        grad_prob = grad_prob_of(gradients_kv_block)
        grad_score = (weights * (grad_prob - row_delta[:, :, None]) * score_scale).astype(
            jnp.bfloat16
        )
        low_weights = weights.astype(jnp.bfloat16)
        grad_query = jnp.einsum(
            "hts,sd->thd",
            grad_score,
            gradients_kv_block[:, :head_width],
            preferred_element_type=jnp.float32,
        )
        grad_key = jnp.einsum(
            "hts,thd->sd", grad_score, queries, preferred_element_type=jnp.float32
        )
        grad_value = jnp.einsum(
            "hts,thd->sd", low_weights, grads_out, preferred_element_type=jnp.float32
        )
        grad_query, share_grads = (
            grad_query,
            jnp.concatenate([grad_key, grad_value], axis=1).astype(jnp.bfloat16),
        )
        query_grads = query_grads + grad_query
        shares.append(share_grads)
    gathered = lax.optimization_barrier(shares[0]).astype(jnp.float32)
    for offset in range(1, HOPS + 1):
        gathered = gathered + shifted(shares[offset], "ctx", -offset).astype(jnp.float32)
    d_query = query_grads.reshape(tok_rows, head_count * head_width).astype(jnp.bfloat16)
    return (d_query, gathered.astype(jnp.bfloat16))


def solution(mesh):
    placed = (P("ctx", "head"), P("ctx", "head"), P("ctx", "head"), P("head"))
    return jax.shard_map(
        shards,
        mesh=mesh,
        in_specs=placed,
        out_specs=(P("ctx", "head"), P("ctx", "head")),
        check_vma=False,
    )
```

profile of v0, /device:TPU:8, one launch (start us, length us, event | category | flops | bytes accessed | tf_op | source)
XLA Modules:
  0.0 121.5 jit_solution(9781181645937956488)
XLA Ops:
  0.6 3.5 %collective-permute-start.1 = (bf16[768,256]{1,0:T(8,128)(2,1)}, bf16[768,256]{1,0:T(8,128)(2,1)S(1)}, u32[]{:S(2)}, u32[]{:S(2)}) collective-permute-start(bf16[768,256]{1,0:T(8,128)(2,1)} %param.5), channel_id=1, source_target_pairs={{0,8},{4,12},{8,16},{12,20},{16,24},{20,28},{1,9},{5,13},{9,17},{1... | collective-permute-start | bytes 1179656 | tf_op jit(solution)/shard_map/ppermute | solution.py:12
  4.1 3.4 %collective-permute-start = (bf16[768,256]{1,0:T(8,128)(2,1)}, bf16[768,256]{1,0:T(8,128)(2,1)S(1)}, u32[]{:S(2)}, u32[]{:S(2)}) collective-permute-start(bf16[768,256]{1,0:T(8,128)(2,1)} %param.5), channel_id=1, source_target_pairs={{0,4},{4,8},{8,12},{12,16},{16,20},{20,24},{24,28},{1,5},{5,9},{9,... | collective-permute-start | bytes 1179656 | tf_op jit(solution)/shard_map/ppermute | solution.py:12
  7.5 3.7 %collective-permute-start.2 = (bf16[768,256]{1,0:T(8,128)(2,1)}, bf16[768,256]{1,0:T(8,128)(2,1)}, u32[]{:S(2)}, u32[]{:S(2)}) collective-permute-start(bf16[768,256]{1,0:T(8,128)(2,1)} %param.5), channel_id=1, source_target_pairs={{0,12},{4,16},{8,20},{12,24},{16,28},{1,13},{5,17},{9,21},{13,25},... | collective-permute-start | bytes 1179656 | tf_op jit(solution)/shard_map/ppermute | solution.py:12
  11.2 1.2 copy.94
  12.4 0.0 copy-start.15
  12.4 0.0 copy-start.18
  12.4 1.3 %copy.95 = bf16[768,256]{0,1:T(8,128)(2,1)S(1)} copy(bf16[768,256]{1,0:T(8,128)(2,1)} %param.6) | data formatting | bytes 786432 | tf_op jit(solution)/shard_map/reshape | solution.py:25
  13.8 0.7 select_reduce_fusion
  14.5 2.1 %compare_and_fusion.2 = (pred[768,768]{0,1:T(8,128)(4,1)S(1)}, pred[768,768]{0,1:T(8,128)(4,1)S(1)}, pred[768,768]{0,1:T(8,128)(4,1)S(1)}, pred[768,768]{0,1:T(8,128)(4,1)S(1)}) fusion(s32[768]{0:T(1024)S(1)} %get-tuple-element.42, s32[768]{0:T(1024)S(1)} %select_reduce_fusion, s32[768]{0:T(1024)S(1)} %get-tuple-element.41, s32[768]{0:T(1024)S(1)} %get-tuple-element.40, ...), kind=kLoop, calls=%fused_computation.73 | loop fusion | flops 7077888 | bytes 2374656 | tf_op jit(solution)/shard_map/and | solution.py:35
  16.7 2.2 %fusion.31 = (f32[2,768]{1,0:T(2,128)S(1)}, f32[768,768,2]{1,0,2:T(8,128)S(1)}) fusion(pred[768,768]{0,1:T(8,128)(4,1)S(1)} %get-tuple-element.26, bf16[768,2,128]{0,2,1:T(8,128)(2,1)S(1)} %bitcast.271, bf16[768,256]{1,0:T(8,128)(2,1)} %param.5), kind=kOutput, calls=%fused_computation.51 | convolution fusion | flops 305527296 | bytes 5904384 | tf_op jit(solution)/shard_map/thd,sd->hts/dot_general | solution.py:41
  18.9 1.8 %fusion.12 = (f32[2,768]{1,0:T(2,128)S(1)}, f32[2,768]{1,0:T(2,128)S(1)}, f32[768,768,2]{1,0,2:T(8,128)S(1)}) fusion(f32[768,768,2]{1,0,2:T(8,128)S(1)} %get-tuple-element.32, f32[2,768]{1,0:T(2,128)S(1)} %get-tuple-element.31, pred[768,768]{0,1:T(8,128)(4,1)S(1)} %get-tuple-element.26, bf16[768,2,128]{0,2,1:T(8,128)(2,1)S(1)} %bitcast.262, ...), kind=kOutput, calls=%fused_computation.20 | convolution fusion | flops 309064704 | bytes 10635264 | tf_op jit(solution)/shard_map/thd,sd->hts/dot_general | solution.py:48
  20.6 3.7 %collective-permute-done = bf16[768,256]{1,0:T(8,128)(2,1)S(1)} collective-permute-done((bf16[768,256]{1,0:T(8,128)(2,1)}, bf16[768,256]{1,0:T(8,128)(2,1)S(1)}, u32[]{:S(2)}, u32[]{:S(2)}) %collective-permute-start) | collective-permute-done | bytes 393248 | tf_op jit(solution)/shard_map/ppermute | solution.py:12
  24.4 1.0 fusion.26
  25.4 0.0 copy-start.16
  25.4 0.0 copy-start.9
  25.4 0.7 copy-done.9
  26.2 2.1 %fusion.21 = (f32[2,768]{1,0:T(2,128)S(1)}, f32[768,768,2]{1,0,2:T(8,128)S(1)}) fusion(pred[768,768]{0,1:T(8,128)(4,1)S(1)} %get-tuple-element.24, bf16[768,2,128]{0,2,1:T(8,128)(2,1)} %bitcast.273, bf16[768,256]{1,0:T(8,128)(2,1)} %copy-done.9), kind=kOutput, calls=%fused_computation.35 | convolution fusion | flops 305527296 | bytes 5904384 | tf_op jit(solution)/shard_map/thd,sd->hts/dot_general | solution.py:41
  28.3 2.0 %fusion.16 = (f32[2,768]{1,0:T(2,128)S(1)}, f32[768,768,2]{1,0,2:T(8,128)S(1)}) fusion(pred[768,768]{0,1:T(8,128)(4,1)S(1)} %get-tuple-element.25, bf16[768,2,128]{0,2,1:T(8,128)(2,1)S(1)} %bitcast.274, bf16[768,256]{1,0:T(8,128)(2,1)} %collective-permute-done.2), kind=kOutput, calls=%fused_computation.27 | convolution fusion | flops 305527296 | bytes 5904384 | tf_op jit(solution)/shard_map/thd,sd->hts/dot_general | solution.py:41
  30.3 0.0 copy-start.10
  30.3 5.1 %fusion = (f32[2,768]{1,0:T(2,128)S(1)}, f32[2,768]{1,0:T(2,128)S(1)}, f32[768,768,2]{1,0,2:T(8,128)}) fusion(f32[768,768,2]{1,0,2:T(8,128)S(1)} %get-tuple-element.28, f32[2,768]{1,0:T(2,128)S(1)} %get-tuple-element.16, pred[768,768]{0,1:T(8,128)(4,1)S(1)} %get-tuple-element.25, bf16[768,2,128]{0,2,1:T(8,128)(2,1)S(1)} %bitcast.263, ...), kind=kOutput, calls=%fused_computation.2 | convolution fusion | flops 309064704 | bytes 10635264 | tf_op jit(solution)/shard_map/thd,sd->hts/dot_general | solution.py:48
  35.5 3.8 %fusion.4 = (f32[2,768]{1,0:T(2,128)S(1)}, f32[2,768]{1,0:T(2,128)S(1)}, f32[768,768,2]{1,0,2:T(8,128)}) fusion(f32[768,768,2]{1,0,2:T(8,128)S(1)} %get-tuple-element.30, f32[2,768]{1,0:T(2,128)S(1)} %get-tuple-element.17, pred[768,768]{0,1:T(8,128)(4,1)S(1)} %get-tuple-element.24, bf16[768,2,128]{0,2,1:T(8,128)(2,1)S(1)} %bitcast.264, ...), kind=kOutput, calls=%fused_computation.8 | convolution fusion | flops 309064704 | bytes 10635264 | tf_op jit(solution)/shard_map/thd,sd->hts/dot_general | solution.py:48
  39.3 3.9 %fusion.8 = (f32[2,768]{1,0:T(2,128)S(1)}, f32[2,768]{1,0:T(2,128)S(1)}, f32[768,768,2]{1,0,2:T(8,128)}) fusion(f32[768,768,2]{1,0,2:T(8,128)S(1)} %get-tuple-element.34, f32[2,768]{1,0:T(2,128)S(1)} %get-tuple-element.18, pred[768,768]{0,1:T(8,128)(4,1)S(1)} %get-tuple-element.23, bf16[768,2,128]{0,2,1:T(8,128)(2,1)S(1)} %bitcast.265, ...), kind=kOutput, calls=%fused_computation.14 | convolution fusion | flops 309064704 | bytes 10635264 | tf_op jit(solution)/shard_map/thd,sd->hts/dot_general | solution.py:48
  43.2 2.0 %fusion.83 = bf16[768,128]{0,1:T(8,128)(2,1)} fusion(bf16[768,2,128]{0,2,1:T(8,128)(2,1)S(1)} %bitcast.266, f32[768,768,2]{1,0,2:T(8,128)S(1)} %get-tuple-element.32, f32[2,768]{1,0:T(2,128)S(1)} %get-tuple-element.14, pred[768,768]{0,1:T(8,128)(4,1)S(1)} %get-tuple-element.26), kind=kOutput, calls=%fused_computation.95 | convolution fusion | flops 306806784 | bytes 5904384 | tf_op jit(solution)/shard_map/hts,thd->sd/dot_general | solution.py:96
  45.3 2.2 %fusion.80 = bf16[768,128]{0,1:T(8,128)(2,1)} fusion(bf16[768,2,128]{0,2,1:T(8,128)(2,1)S(1)} %bitcast.267, f32[768,768,2]{1,0,2:T(8,128)S(1)} %get-tuple-element.34, f32[2,768]{1,0:T(2,128)S(1)} %get-tuple-element.14, pred[768,768]{0,1:T(8,128)(4,1)S(1)} %get-tuple-element.23), kind=kOutput, calls=%fused_computation.94 | convolution fusion | flops 306806784 | bytes 5904384 | tf_op jit(solution)/shard_map/hts,thd->sd/dot_general | solution.py:96
  47.5 2.0 %fusion.74 = bf16[768,128]{0,1:T(8,128)(2,1)} fusion(bf16[768,2,128]{0,2,1:T(8,128)(2,1)S(1)} %bitcast.268, f32[768,768,2]{1,0,2:T(8,128)S(1)} %get-tuple-element.28, f32[2,768]{1,0:T(2,128)S(1)} %get-tuple-element.14, pred[768,768]{0,1:T(8,128)(4,1)S(1)} %get-tuple-element.25), kind=kOutput, calls=%fused_computation.92 | convolution fusion | flops 306806784 | bytes 5904384 | tf_op jit(solution)/shard_map/hts,thd->sd/dot_general | solution.py:96
  49.5 2.0 %fusion.77 = bf16[768,128]{0,1:T(8,128)(2,1)} fusion(bf16[768,2,128]{0,2,1:T(8,128)(2,1)S(1)} %bitcast.269, f32[768,768,2]{1,0,2:T(8,128)S(1)} %get-tuple-element.30, f32[2,768]{1,0:T(2,128)S(1)} %get-tuple-element.14, pred[768,768]{0,1:T(8,128)(4,1)S(1)} %get-tuple-element.24), kind=kOutput, calls=%fused_computation.93 | convolution fusion | flops 306806784 | bytes 5904384 | tf_op jit(solution)/shard_map/hts,thd->sd/dot_general | solution.py:96
  51.6 0.0 copy-start.17
  51.6 14.1 %fusion.7 = (bf16[2,768,768]{1,2,0:T(8,128)(2,1)}, bf16[2,768,768]{1,2,0:T(8,128)(2,1)}, bf16[2,768,768]{1,2,0:T(8,128)(2,1)}, bf16[2,768,768]{1,2,0:T(8,128)(2,1)}) fusion(f32[768,768,2]{1,0,2:T(8,128)} %get-tuple-element.36, f32[768,768,2]{1,0,2:T(8,128)S(1)} %get-tuple-element.30, f32[2,768]{1,0:T(2,128)S(1)} %add_divide_fusion, ...), kind=kLoop, calls=%fused_computation.11 | loop fusion | flops 33030144 | bytes 49557504 | tf_op jit(solution)/shard_map/convert_element_type | solution.py:83
  65.8 3.4 %fusion.72 = bf16[768,128]{0,1:T(8,128)(2,1)} fusion(bf16[2,768,768]{1,2,0:T(8,128)(2,1)} %get-tuple-element.19, bf16[768,2,128]{0,2,1:T(8,128)(2,1)S(1)} %bitcast.275), kind=kOutput, calls=%fused_computation.90 | convolution fusion | flops 302088192 | bytes 2949120 | tf_op jit(solution)/shard_map/hts,thd->sd/dot_general | solution.py:93
  69.2 1.6 %fusion.71 = bf16[768,128]{0,1:T(8,128)(2,1)} fusion(bf16[2,768,768]{1,2,0:T(8,128)(2,1)S(1)} %copy-done.4, bf16[768,2,128]{0,2,1:T(8,128)(2,1)S(1)} %bitcast.276), kind=kOutput, calls=%fused_computation.89 | convolution fusion | flops 302088192 | bytes 2949120 | tf_op jit(solution)/shard_map/hts,thd->sd/dot_general | solution.py:93
  70.8 1.6 %fusion.73 = bf16[768,128]{0,1:T(8,128)(2,1)} fusion(bf16[2,768,768]{1,2,0:T(8,128)(2,1)S(1)} %copy-done.3, bf16[768,2,128]{0,2,1:T(8,128)(2,1)S(1)} %bitcast.277), kind=kOutput, calls=%fused_computation.91 | convolution fusion | flops 302088192 | bytes 2949120 | tf_op jit(solution)/shard_map/hts,thd->sd/dot_general | solution.py:93
  72.4 0.5 fusion.91
  72.9 1.7 %fusion.100 = f32[2,768,128]{1,2,0:T(8,128)S(1)} fusion(bf16[2,768,768]{1,2,0:T(8,128)(2,1)S(1)} %copy-done.3, bf16[768,256]{1,0:T(8,128)(2,1)} %collective-permute-done.2), kind=kOutput, calls=%fused_computation.121 | convolution fusion | flops 301989888 | bytes 3342336 | tf_op jit(solution)/shard_map/hts,sd->thd/dot_general | solution.py:87
  74.6 0.5 convolution_add_fusion.1
  75.2 0.5 fusion.57
  75.7 0.9 copy.72
  76.7 1.0 pad_maximum_fusion.3
  77.7 1.3 %collective-permute-start.5 = (bf16[768,256]{0,1:T(8,128)(2,1)S(1)}, bf16[768,256]{0,1:T(8,128)(2,1)S(1)}, u32[]{:S(2)}, u32[]{:S(2)}) collective-permute-start(bf16[768,256]{0,1:T(8,128)(2,1)S(1)} %pad_maximum_fusion.3), channel_id=1, source_target_pairs={{12,0},{16,4},{20,8},{24,12},{28,16},{13,1},{17,5},{21,9},{25,13},... | collective-permute-start | bytes 1179656 | tf_op jit(solution)/shard_map/ppermute | solution.py:12
  79.0 1.0 pad_maximum_fusion.1
  80.1 4.7 %collective-permute-start.3 = (bf16[768,256]{0,1:T(8,128)(2,1)S(1)}, bf16[768,256]{0,1:T(8,128)(2,1)S(1)}, u32[]{:S(2)}, u32[]{:S(2)}) collective-permute-start(bf16[768,256]{0,1:T(8,128)(2,1)S(1)} %pad_maximum_fusion.1), channel_id=1, source_target_pairs={{4,0},{8,4},{12,8},{16,12},{20,16},{24,20},{28,24},{5,1},{9,5},{13... | collective-permute-start | bytes 1179656 | tf_op jit(solution)/shard_map/ppermute | solution.py:12
  84.7 1.0 pad_maximum_fusion.2
  85.8 1.9 %collective-permute-start.4 = (bf16[768,256]{0,1:T(8,128)(2,1)S(1)}, bf16[768,256]{0,1:T(8,128)(2,1)S(1)}, u32[]{:S(2)}, u32[]{:S(2)}) collective-permute-start(bf16[768,256]{0,1:T(8,128)(2,1)S(1)} %pad_maximum_fusion.2), channel_id=1, source_target_pairs={{8,0},{12,4},{16,8},{20,12},{24,16},{28,20},{9,1},{13,5},{17,9},{2... | collective-permute-start | bytes 1179656 | tf_op jit(solution)/shard_map/ppermute | solution.py:12
  87.7 0.9 fusion.70
  88.7 1.7 %collective-permute-done.5 = bf16[768,256]{0,1:T(8,128)(2,1)S(1)} collective-permute-done((bf16[768,256]{0,1:T(8,128)(2,1)S(1)}, bf16[768,256]{0,1:T(8,128)(2,1)S(1)}, u32[]{:S(2)}, u32[]{:S(2)}) %collective-permute-start.5) | collective-permute-done | bytes 393248 | tf_op jit(solution)/shard_map/ppermute | solution.py:12
  90.3 11.7 %collective-permute-done.3 = bf16[768,256]{0,1:T(8,128)(2,1)S(1)} collective-permute-done((bf16[768,256]{0,1:T(8,128)(2,1)S(1)}, bf16[768,256]{0,1:T(8,128)(2,1)S(1)}, u32[]{:S(2)}, u32[]{:S(2)}) %collective-permute-start.3) | collective-permute-done | bytes 393248 | tf_op jit(solution)/shard_map/ppermute | solution.py:12
  102.1 18.3 %collective-permute-done.4 = bf16[768,256]{0,1:T(8,128)(2,1)S(1)} collective-permute-done((bf16[768,256]{0,1:T(8,128)(2,1)S(1)}, bf16[768,256]{0,1:T(8,128)(2,1)S(1)}, u32[]{:S(2)}, u32[]{:S(2)}) %collective-permute-start.4) | collective-permute-done | bytes 393248 | tf_op jit(solution)/shard_map/ppermute | solution.py:12
  120.4 0.2 add_convert_fusion
  120.6 0.9 copy.73
  (43 shorter events, 0.2 us)
Async XLA Ops:
  0.6 24.8 %collective-permute-start.1 = (bf16[768,256]{1,0:T(8,128)(2,1)}, bf16[768,256]{1,0:T(8,128)(2,1)S(1)}, u32[]{:S(2)}, u32[]{:S(2)}) collective-permute-start(bf16[768,256]{1,0:T(8,128)(2,1)} %param.5), channel_id=1, source_target_pairs={{0,8},{4,12},{8,16},{12,20},{16,24},{20,28},{1,9},{5,13},{9,17},{1... | collective-permute-start | bytes 1179656 | tf_op jit(solution)/shard_map/ppermute | solution.py:12
  4.1 20.2 %collective-permute-start = (bf16[768,256]{1,0:T(8,128)(2,1)}, bf16[768,256]{1,0:T(8,128)(2,1)S(1)}, u32[]{:S(2)}, u32[]{:S(2)}) collective-permute-start(bf16[768,256]{1,0:T(8,128)(2,1)} %param.5), channel_id=1, source_target_pairs={{0,4},{4,8},{8,12},{12,16},{16,20},{20,24},{24,28},{1,5},{5,9},{9,... | collective-permute-start | bytes 1179656 | tf_op jit(solution)/shard_map/ppermute | solution.py:12
  7.5 20.8 %collective-permute-start.2 = (bf16[768,256]{1,0:T(8,128)(2,1)}, bf16[768,256]{1,0:T(8,128)(2,1)}, u32[]{:S(2)}, u32[]{:S(2)}) collective-permute-start(bf16[768,256]{1,0:T(8,128)(2,1)} %param.5), channel_id=1, source_target_pairs={{0,12},{4,16},{8,20},{12,24},{16,28},{1,13},{5,17},{9,21},{13,25},... | collective-permute-start | bytes 1179656 | tf_op jit(solution)/shard_map/ppermute | solution.py:12
  12.4 11.9 %copy-start.15 = (bf16[768,256]{0,1:T(8,128)(2,1)}, bf16[768,256]{0,1:T(8,128)(2,1)S(1)}, u32[]{:S(2)}) copy-start(bf16[768,256]{0,1:T(8,128)(2,1)S(1)} %copy.94) | copy-start | bytes 1179652
  12.4 6.4 %copy-start.18 = (bf16[768,256]{1,0:T(8,128)(2,1)S(1)}, bf16[768,256]{1,0:T(8,128)(2,1)}, u32[]{:S(2)}) copy-start(bf16[768,256]{1,0:T(8,128)(2,1)} %param.5) | copy-start | bytes 1179652
  16.6 26.6 %copy-start.8 = (pred[768,768]{0,1:T(8,128)(4,1)}, pred[768,768]{0,1:T(8,128)(4,1)S(1)}, u32[]{:S(2)}) copy-start(pred[768,768]{0,1:T(8,128)(4,1)S(1)} %get-tuple-element.26) | copy-start | bytes 1769476
  16.7 28.6 %copy-start.5 = (pred[768,768]{0,1:T(8,128)(4,1)}, pred[768,768]{0,1:T(8,128)(4,1)S(1)}, u32[]{:S(2)}) copy-start(pred[768,768]{0,1:T(8,128)(4,1)S(1)} %get-tuple-element.23) | copy-start | bytes 1769476
  16.7 30.8 %copy-start.7 = (pred[768,768]{0,1:T(8,128)(4,1)}, pred[768,768]{0,1:T(8,128)(4,1)S(1)}, u32[]{:S(2)}) copy-start(pred[768,768]{0,1:T(8,128)(4,1)S(1)} %get-tuple-element.25) | copy-start | bytes 1769476
  16.7 32.8 %copy-start.6 = (pred[768,768]{0,1:T(8,128)(4,1)}, pred[768,768]{0,1:T(8,128)(4,1)S(1)}, u32[]{:S(2)}) copy-start(pred[768,768]{0,1:T(8,128)(4,1)S(1)} %get-tuple-element.24) | copy-start | bytes 1769476
  24.3 1.1 copy-start.12
  25.4 2.9 %copy-start.16 = (bf16[768,256]{0,1:T(8,128)(2,1)S(1)}, bf16[768,256]{0,1:T(8,128)(2,1)}, u32[]{:S(2)}) copy-start(bf16[768,256]{0,1:T(8,128)(2,1)} %copy-done.15) | copy-start | bytes 1179652
  25.4 0.7 copy-start.9
  30.3 17.2 %copy-start = (f32[768,768,2]{1,0,2:T(8,128)}, f32[768,768,2]{1,0,2:T(8,128)S(1)}, u32[]{:S(2)}) copy-start(f32[768,768,2]{1,0,2:T(8,128)S(1)} %get-tuple-element.28) | copy-start | bytes 14155780
  30.3 5.1 %copy-start.10 = (bf16[768,256]{1,0:T(8,128)(2,1)S(1)}, bf16[768,256]{1,0:T(8,128)(2,1)}, u32[]{:S(2)}) copy-start(bf16[768,256]{1,0:T(8,128)(2,1)} %copy-done.9) | copy-start | bytes 1179652
  35.4 3.8 %copy-start.13 = (bf16[768,256]{1,0:T(8,128)(2,1)S(1)}, bf16[768,256]{1,0:T(8,128)(2,1)}, u32[]{:S(2)}) copy-start(bf16[768,256]{1,0:T(8,128)(2,1)} %copy-done.12) | copy-start | bytes 1179652
  51.6 14.2 %copy-start.17 = (bf16[768,256]{0,1:T(8,128)(2,1)S(1)}, bf16[768,256]{0,1:T(8,128)(2,1)}, u32[]{:S(2)}) copy-start(bf16[768,256]{0,1:T(8,128)(2,1)} %copy-done.15) | copy-start | bytes 1179652
  65.8 3.4 %copy-start.4 = (bf16[2,768,768]{1,2,0:T(8,128)(2,1)S(1)}, bf16[2,768,768]{1,2,0:T(8,128)(2,1)}, u32[]{:S(2)}) copy-start(bf16[2,768,768]{1,2,0:T(8,128)(2,1)} %get-tuple-element.20) | copy-start | bytes 7077892
  65.8 5.0 %copy-start.3 = (bf16[2,768,768]{1,2,0:T(8,128)(2,1)S(1)}, bf16[2,768,768]{1,2,0:T(8,128)(2,1)}, u32[]{:S(2)}) copy-start(bf16[2,768,768]{1,2,0:T(8,128)(2,1)} %get-tuple-element.21) | copy-start | bytes 7077892
  69.2 3.2 %copy-start.1 = (bf16[2,768,768]{1,2,0:T(8,128)(2,1)S(1)}, bf16[2,768,768]{1,2,0:T(8,128)(2,1)}, u32[]{:S(2)}) copy-start(bf16[2,768,768]{1,2,0:T(8,128)(2,1)} %get-tuple-element.22) | copy-start | bytes 7077892
  69.2 3.2 %copy-start.19 = (bf16[768,256]{1,0:T(8,128)(2,1)S(1)}, bf16[768,256]{1,0:T(8,128)(2,1)}, u32[]{:S(2)}) copy-start(bf16[768,256]{1,0:T(8,128)(2,1)} %param.5) | copy-start | bytes 1179652
  70.8 3.9 %copy-start.14 = (bf16[768,256]{1,0:T(8,128)(2,1)S(1)}, bf16[768,256]{1,0:T(8,128)(2,1)}, u32[]{:S(2)}) copy-start(bf16[768,256]{1,0:T(8,128)(2,1)} %copy-done.12) | copy-start | bytes 1179652
  72.3 2.8 %copy-start.2 = (bf16[2,768,768]{1,2,0:T(8,128)(2,1)S(1)}, bf16[2,768,768]{1,2,0:T(8,128)(2,1)}, u32[]{:S(2)}) copy-start(bf16[2,768,768]{1,2,0:T(8,128)(2,1)} %get-tuple-element.19) | copy-start | bytes 7077892
  72.3 2.8 %copy-start.11 = (bf16[768,256]{1,0:T(8,128)(2,1)S(1)}, bf16[768,256]{1,0:T(8,128)(2,1)}, u32[]{:S(2)}) copy-start(bf16[768,256]{1,0:T(8,128)(2,1)} %copy-done.9) | copy-start | bytes 1179652
  75.7 12.9 %copy-start.20 = (bf16[768,128]{0,1:T(8,128)(2,1)S(1)}, bf16[768,128]{0,1:T(8,128)(2,1)}, u32[]{:S(2)}) copy-start(bf16[768,128]{0,1:T(8,128)(2,1)} %fusion.83) | copy-start | bytes 589828
  77.7 12.6 %collective-permute-start.5 = (bf16[768,256]{0,1:T(8,128)(2,1)S(1)}, bf16[768,256]{0,1:T(8,128)(2,1)S(1)}, u32[]{:S(2)}, u32[]{:S(2)}) collective-permute-start(bf16[768,256]{0,1:T(8,128)(2,1)S(1)} %pad_maximum_fusion.3), channel_id=1, source_target_pairs={{12,0},{16,4},{20,8},{24,12},{28,16},{13,1},{17,5},{21,9},{25,13},... | collective-permute-start | bytes 1179656 | tf_op jit(solution)/shard_map/ppermute | solution.py:12
  80.1 22.0 %collective-permute-start.3 = (bf16[768,256]{0,1:T(8,128)(2,1)S(1)}, bf16[768,256]{0,1:T(8,128)(2,1)S(1)}, u32[]{:S(2)}, u32[]{:S(2)}) collective-permute-start(bf16[768,256]{0,1:T(8,128)(2,1)S(1)} %pad_maximum_fusion.1), channel_id=1, source_target_pairs={{4,0},{8,4},{12,8},{16,12},{20,16},{24,20},{28,24},{5,1},{9,5},{13... | collective-permute-start | bytes 1179656 | tf_op jit(solution)/shard_map/ppermute | solution.py:12
  85.8 34.6 %collective-permute-start.4 = (bf16[768,256]{0,1:T(8,128)(2,1)S(1)}, bf16[768,256]{0,1:T(8,128)(2,1)S(1)}, u32[]{:S(2)}, u32[]{:S(2)}) collective-permute-start(bf16[768,256]{0,1:T(8,128)(2,1)S(1)} %pad_maximum_fusion.2), channel_id=1, source_target_pairs={{8,0},{12,4},{16,8},{20,12},{24,16},{28,20},{9,1},{13,5},{17,9},{2... | collective-permute-start | bytes 1179656 | tf_op jit(solution)/shard_map/ppermute | solution.py:12
where the time goes:
time: 122 us
  matrix products  41 us (34%)
  waiting for transfers between devices  35.5 us (29%)
  other arithmetic  20.4 us (17%)
  starting transfers between devices  18.5 us (15%)
  local copies, waits for them, and re-layouts  5.15 us (4%)
    ppermute x6, waiting for transfers between devices, shifted(): lax.ppermute(value, axis, [(source, source + steps) for source in range(f...  35.5 us
    ppermute x6, starting transfers between devices, shifted(): lax.ppermute(value, axis, [(source, source + steps) for source in range(f...  18.5 us
    dot_general x4, matrix products, grad_prob_of(): jnp.einsum('thd,sd->hts', grads_out, kv_block[:, head_width:], preferred_...  14.6 us
    convert_element_type x1, other arithmetic, shards(): (weights * (grad_prob - row_delta[:, :, None]) * score_scale).astype(jnp....  14.1 us
    dot_general x4, matrix products, shards(): jnp.einsum('hts,thd->sd', low_weights, grads_out, preferred_element_type=...  8.32 us
    dot_general x4, matrix products, shards(): jnp.einsum('hts,thd->sd', grad_score, queries, preferred_element_type=jnp...  7.44 us
    dot_general x4, matrix products, scores_of(): jnp.einsum('thd,sd->hts', queries, kv_block[:, :head_width], preferred_el...  7.29 us
    dot_general x4, matrix products, shards(): jnp.einsum('hts,sd->thd', grad_score, gradients_kv_block[:, :head_width],...  3.31 us
  transfers between devices with their start and end apart: 6, of which 4 were waited for; matrix products, arithmetic and copies ran while one was open for 13% of the time, Pallas kernels for 0%

commit v1 on v0

v1 whole, which is shorter than its diff:
```python
import functools
import math

import jax
import jax.numpy as jnp
from jax import lax
from jax.experimental import pallas as pl
from jax.experimental.pallas import tpu as pltpu
from jax.sharding import PartitionSpec as P

HOPS = 3
NEG = -1e30
SUB = 2
KEY_TILES = 4
MESH = pl.DeviceIdType.MESH


def dot_nt(a, b):
    return lax.dot_general(a, b, (((1,), (1,)), ((), ())), preferred_element_type=jnp.float32)


def dot(a, b):
    return jnp.dot(a, b, preferred_element_type=jnp.float32)


def kernel(
    n, q_ref, g_ref, kv_ref, ds_ref, dq_ref, dkv_ref,
    got, expo, gprob, top, total, weighted, factor, delta, low_p, low_g, dq_t, own, share, back,
    own_rows, f_send, f_recv, b_send, b_recv,
):
    me = lax.axis_index("ctx")
    odd = lax.rem(me, 2)
    is_odd, is_even = odd == 1, odd == 0
    tok, width = q_ref.shape
    hd = kv_ref.shape[1] // 2
    heads = width // hd
    half = tok // 2
    piece = half // SUB
    kt_rows = tok // KEY_TILES
    qt = math.gcd(tok, 256)
    scale = hd ** -0.5
    to_log2 = scale * math.log2(math.e)
    has_next = me + 2 < n

    barrier = pltpu.get_barrier_semaphore()
    pair = me + 1 - 2 * odd

    def greet(device):
        pl.semaphore_signal(barrier, inc=1, device_id={"ctx": device}, device_id_type=MESH)

    greet(pair)

    @pl.when(has_next)
    def _():
        greet(me + 2)

    @pl.when(me >= 2)
    def _():
        greet(me - 2)

    @pl.when(has_next & (me >= 2))
    def _():
        pl.semaphore_wait(barrier, 3)

    @pl.when(jnp.logical_not(has_next & (me >= 2)))
    def _():
        pl.semaphore_wait(barrier, 2)

    def rows_of(c):
        return pl.ds(c * piece, piece)

    FIRST, SECOND = range(SUB), range(SUB, 2 * SUB)
    ALL = range(2 * SUB)

    def fwd(slot, src, device, t, c):
        return pltpu.make_async_remote_copy(
            src_ref=src.at[rows_of(c)], dst_ref=got.at[t - 1, rows_of(c)],
            send_sem=f_send.at[slot, c], recv_sem=f_recv.at[t - 1, c],
            device_id={"ctx": device}, device_id_type=MESH,
        )

    def arrived(t, c):
        fwd(0, kv_ref, pair, t, c).wait_recv()

    def when(cond, f):
        pl.when(cond)(f)

    @pl.when(is_even)
    def _():
        for c in list(SECOND) + list(FIRST):
            fwd(0, kv_ref, me + 1, 1, c).start()

        @pl.when(has_next)
        def _():
            for c in FIRST:
                fwd(1, kv_ref, me + 2, 2, c).start()

    @pl.when(is_odd & has_next)
    def _():
        for c in ALL:
            fwd(1, kv_ref, me + 2, 2, c).start()

    position = me * tok + lax.broadcasted_iota(jnp.int32, (1, tok), 1)
    owners = jnp.zeros((1, tok), jnp.int32)
    for i in range(ds_ref.shape[0]):
        start = ds_ref[i]
        owners = jnp.maximum(owners, jnp.where(position >= start, start, 0))
    own_rows[...] = owners
    top[...] = jnp.full(top.shape, NEG, jnp.float32)
    total[...] = jnp.zeros_like(total)
    weighted[...] = jnp.zeros_like(weighted)
    dq_t[...] = jnp.zeros_like(dq_t)

    def tiles():
        for h in range(heads):
            for j in range(tok // qt):
                yield h, j, slice(j * qt, (j + 1) * qt), slice(h * hd, (h + 1) * hd), slice(
                    h * tok + j * qt, h * tok + (j + 1) * qt)

    def block(t):
        return kv_ref if t == 0 else got.at[t - 1]

    def absorb(t, kt):
        r0 = kt * kt_rows
        rows = slice(r0, r0 + kt_rows)
        src = block(t)
        k, v = src[rows, :hd], src[rows, hd:]
        base = (me - t) * tok + r0
        stat = t * KEY_TILES + kt
        key_row = lax.broadcasted_iota(jnp.int32, (kt_rows, qt), 0)
        for h, j, qrows, cols, flat in tiles():
            if t == 0 and (j + 1) * qt <= r0:
                continue
            s = dot_nt(k, q_ref[qrows, cols]) * to_log2
            gp = dot_nt(v, g_ref[qrows, cols]) * scale
            visible = key_row >= own_rows[:, qrows] - base
            if t == 0:
                query_row = lax.broadcasted_iota(jnp.int32, (1, qt), 1) + (j * qt - r0)
                visible = visible & (key_row <= query_row)
            s = jnp.where(visible, s, NEG)
            m = jnp.max(s, axis=0, keepdims=True)
            e = jnp.exp2(s - m)
            expo[t, rows, flat] = e
            gprob[t, rows, flat] = gp
            top[stat : stat + 1, flat] = m
            total[stat : stat + 1, flat] = jnp.sum(e, axis=0, keepdims=True)
            weighted[stat : stat + 1, flat] = jnp.sum(e * gp, axis=0, keepdims=True)

    per_half = KEY_TILES // 2

    def absorb_half(t, which):
        def run():
            for kt in range(which * per_half, (which + 1) * per_half):
                absorb(t, kt)

        if t == 0:
            run()
        else:
            when(me >= t, run)

    absorb_half(0, 0)
    absorb_half(0, 1)

    @pl.when(is_even & (me >= 2))
    def _():
        for c in FIRST:
            arrived(2, c)
            fwd(3, got.at[1], me + 1, 3, c).start()

    @pl.when(is_odd)
    def _():
        for i in range(SUB):
            arrived(1, SECOND[i])

            @pl.when(has_next)
            def _():
                fwd(2, got.at[0], me + 2, 3, SECOND[i]).start()

            @pl.when(me >= 2)
            def _():
                arrived(2, FIRST[i])
                fwd(3, got.at[1], me - 1, 1, FIRST[i]).start()

    absorb_half(2, 0)

    @pl.when(is_odd)
    def _():
        @pl.when(me >= 2)
        def _():
            for c in SECOND:
                arrived(2, c)
                fwd(3, got.at[1], me - 1, 1, c).start()

        for c in FIRST:
            arrived(1, c)

    def relay_first(chunks):
        @pl.when(is_even & (me >= 2))
        def _():
            for c in chunks:
                arrived(1, c)

                @pl.when(has_next)
                def _():
                    fwd(2, got.at[0], me + 2, 3, c).start()

    relay_first(FIRST)
    absorb_half(1, 0)
    relay_first(SECOND)
    absorb_half(1, 1)

    @pl.when(is_odd & (me >= 3))
    def _():
        for c in SECOND:
            arrived(3, c)
            fwd(4, got.at[2], me - 1, 2, c).start()

    @pl.when(me >= 3)
    def _():
        for c in FIRST:
            arrived(3, c)

    @pl.when(is_odd & (me >= 3))
    def _():
        absorb_half(2, 1)

    @pl.when(me >= 3)
    def _():
        absorb_half(3, 0)

    @pl.when(is_even & (me >= 2))
    def _():
        for c in SECOND:
            arrived(2, c)
        absorb_half(2, 1)

    @pl.when(is_even & (me >= 3))
    def _():
        for c in SECOND:
            arrived(3, c)

    absorb_half(3, 1)

    best = jnp.max(top[...], axis=0, keepdims=True)
    grow = jnp.exp2(top[...] - best)
    inverse = 1.0 / jnp.sum(grow * total[...], axis=0, keepdims=True)
    factor[...] = grow * inverse
    delta[...] = jnp.sum(grow * weighted[...], axis=0, keepdims=True) * inverse

    def gradients(t, kt):
        r0 = kt * kt_rows
        rows = slice(r0, r0 + kt_rows)
        slot = kt % 2
        stat = t * KEY_TILES + kt
        first = (r0 // qt) * qt if t == 0 else 0
        for h, j, qrows, cols, flat in tiles():
            if j * qt < first:
                continue
            p = expo[t, rows, flat] * factor[stat : stat + 1, flat]
            low_p[slot, :, flat] = p.astype(jnp.bfloat16)
            low_g[slot, :, flat] = (p * (gprob[t, rows, flat] - delta[:, flat])).astype(jnp.bfloat16)
        dk = dv = None
        k_t = block(t)[rows, :hd].T
        for h in range(heads):
            flat = slice(h * tok + first, (h + 1) * tok)
            cols = slice(h * hd, (h + 1) * hd)
            gs = low_g[slot, :, flat]
            dk_h = dot(gs, q_ref[first:, cols])
            dv_h = dot(low_p[slot, :, flat], g_ref[first:, cols])
            dk = dk_h if dk is None else dk + dk_h
            dv = dv_h if dv is None else dv + dv_h
            dq_t[:, flat] += dot(k_t, gs)
        if t == 0:
            own[rows, :hd] = dk
            own[rows, hd:] = dv
        else:
            share[t - 1, rows, :hd] = dk.astype(jnp.bfloat16)
            share[t - 1, rows, hd:] = dv.astype(jnp.bfloat16)

    def gradients_half(t, which):
        def run():
            for kt in range(which * per_half, (which + 1) * per_half):
                gradients(t, kt)

        if t == 0:
            run()
        else:
            when(me >= t, run)

    def bwd(t, device, slot, c):
        return pltpu.make_async_remote_copy(
            src_ref=share.at[t - 1, rows_of(c)], dst_ref=back.at[slot, rows_of(c)],
            send_sem=b_send.at[t - 1, c], recv_sem=b_recv.at[slot, c],
            device_id={"ctx": device}, device_id_type=MESH,
        )

    def returned(slot, c):
        bwd(1, pair, slot, c).wait_recv()

    def merge(t, c):
        returned(t - 1, c)
        rows = rows_of(c)
        both = share[t - 1, rows, :].astype(jnp.float32) + back[t - 1, rows, :].astype(jnp.float32)
        share[t - 1, rows, :] = both.astype(jnp.bfloat16)

    gradients_half(3, 0)

    @pl.when(me >= 3)
    def _():
        @pl.when(is_even)
        def _():
            for c in FIRST:
                bwd(3, me - 2, 0, c).start()

        @pl.when(is_odd)
        def _():
            for c in FIRST:
                bwd(3, me - 1, 1, c).start()

    gradients_half(2, 1)

    @pl.when(is_even & (me >= 2))
    def _():
        for c in SECOND:
            bwd(2, me + 1, 2, c).start()

    gradients_half(3, 1)

    @pl.when(me >= 3)
    def _():
        @pl.when(is_even)
        def _():
            for c in SECOND:
                bwd(3, me - 2, 0, c).start()

        @pl.when(is_odd)
        def _():
            for c in SECOND:
                merge(3, c)
                bwd(3, me - 2, 0, c).start()

    gradients_half(2, 0)

    @pl.when(is_even & (me >= 2))
    def _():
        for c in FIRST:
            merge(2, c)
            bwd(2, me - 2, 4, c).start()

    def send_one(chunks, add_odd):
        @pl.when(is_even & (me >= 2))
        def _():
            for c in chunks:
                @pl.when(has_next)
                def _():
                    merge(1, c)

                bwd(1, me + 1, 1, c).start()

        @pl.when(is_odd)
        def _():
            for c in chunks:
                if add_odd:
                    @pl.when(has_next)
                    def _():
                        merge(1, c)

                bwd(1, me - 1, 3, c).start()

    gradients_half(1, 0)
    send_one(FIRST, False)
    gradients_half(1, 1)
    send_one(SECOND, True)
    gradients_half(0, 0)
    gradients_half(0, 1)

    @pl.when(is_odd & (me >= 2))
    def _():
        for c in ALL:
            merge(2, c)
            bwd(2, me - 2, 4, c).start()

    for h in range(heads):
        dq_ref[:, h * hd : (h + 1) * hd] = dq_t[:, h * tok : (h + 1) * tok].T.astype(jnp.bfloat16)

    def add_back(slot, c):
        returned(slot, c)
        rows = rows_of(c)
        own[rows, :] += back[slot, rows, :].astype(jnp.float32)

    @pl.when(is_even)
    def _():
        for c in ALL:
            add_back(3, c)

        @pl.when(has_next)
        def _():
            for c in FIRST:
                add_back(4, c)

    @pl.when(is_odd & has_next)
    def _():
        for c in ALL:
            add_back(4, c)

    dkv_ref[...] = own[...].astype(jnp.bfloat16)

    def sent(slot, chunks):
        for c in chunks:
            fwd(slot, kv_ref, pair, 1, c).wait_send()

    def sent_back(t, chunks):
        for c in chunks:
            bwd(t, pair, 0, c).wait_send()

    @pl.when(is_even)
    def _():
        sent(0, ALL)

        @pl.when(has_next)
        def _():
            sent(1, FIRST)

        @pl.when(me >= 2)
        def _():
            sent(3, FIRST)

            @pl.when(has_next)
            def _():
                sent(2, ALL)

    @pl.when(is_odd)
    def _():
        @pl.when(has_next)
        def _():
            sent(1, ALL)
            sent(2, SECOND)

        @pl.when(me >= 2)
        def _():
            sent(3, ALL)
            sent(4, SECOND)

    for t in range(1, HOPS + 1):
        when(me >= t, functools.partial(sent_back, t, ALL))


def shards(n, query, key_value, d_out, doc_starts):
    tok, width = query.shape
    hd = key_value.shape[1] // 2
    flat = tok * (width // hd)
    blocks = HOPS + 1
    stats = blocks * KEY_TILES
    bf16, f32 = jnp.bfloat16, jnp.float32
    vmem = pl.BlockSpec(memory_space=pltpu.VMEM)
    pieces = 2 * SUB
    return pl.pallas_call(
        functools.partial(kernel, n),
        out_shape=(
            jax.ShapeDtypeStruct(query.shape, bf16),
            jax.ShapeDtypeStruct(key_value.shape, bf16),
        ),
        in_specs=[vmem, vmem, vmem, pl.BlockSpec(memory_space=pltpu.SMEM)],
        out_specs=(vmem, vmem),
        scratch_shapes=[
            pltpu.VMEM((HOPS, tok, 2 * hd), bf16),
            pltpu.VMEM((blocks, tok, flat), f32),
            pltpu.VMEM((blocks, tok, flat), f32),
            pltpu.VMEM((stats, flat), f32),
            pltpu.VMEM((stats, flat), f32),
            pltpu.VMEM((stats, flat), f32),
            pltpu.VMEM((stats, flat), f32),
            pltpu.VMEM((1, flat), f32),
            pltpu.VMEM((2, tok // KEY_TILES, flat), bf16),
            pltpu.VMEM((2, tok // KEY_TILES, flat), bf16),
            pltpu.VMEM((hd, flat), f32),
            pltpu.VMEM((tok, 2 * hd), f32),
            pltpu.VMEM((HOPS, tok, 2 * hd), bf16),
            pltpu.VMEM((5, tok, 2 * hd), bf16),
            pltpu.VMEM((1, tok), jnp.int32),
            pltpu.SemaphoreType.DMA((5, pieces)),
            pltpu.SemaphoreType.DMA((HOPS, pieces)),
            pltpu.SemaphoreType.DMA((HOPS, pieces)),
            pltpu.SemaphoreType.DMA((5, pieces)),
        ],
        compiler_params=pltpu.CompilerParams(
            collective_id=0, has_side_effects=True, vmem_limit_bytes=63 * 2**20
        ),
    )(query, d_out, key_value, doc_starts)


def solution(mesh):
    placed = (P("ctx", "head"), P("ctx", "head"), P("ctx", "head"), P("head"))
    return jax.shard_map(
        functools.partial(shards, mesh.shape["ctx"]),
        mesh=mesh,
        in_specs=placed,
        out_specs=(P("ctx", "head"), P("ctx", "head")),
        check_vma=False,
    )
```

time: 122 us -> 50.4 us (0.41)
  the two profiles are of different devices: /device:TPU:8 before, /device:TPU:10 now
where the time goes in v1:
time: 50.4 us; the launch traced here: 50.2 us
  Pallas kernels  46.9 us (93%)
  local copies, waits for them, and re-layouts  2.57 us (5%)
  between operations  0.65 us (1%)
    pallas_call x1, Pallas kernels, shards(): pl.pallas_call(functools.partial(kernel, n), out_shape=(jax.ShapeDtypeStr...  46.9 us
    unnamed x4, local copies, waits for them, and re-layouts  2.57 us

profile of v1, /device:TPU:10, one launch (start us, length us, event | category | flops | bytes accessed | tf_op | source)
XLA Modules:
  0.0 50.2 jit_solution(8519309352578596163)
XLA Ops:
  0.6 46.9 %shard_map.59 = (bf16[768,256]{1,0:T(8,128)(2,1)}, bf16[768,256]{1,0:T(8,128)(2,1)}) custom-call(bf16[768,256]{1,0:T(8,128)(2,1)} %q_ref.1, bf16[768,256]{1,0:T(8,128)(2,1)} %g_ref.1, bf16[768,256]{1,0:T(8,128)(2,1)} %kv_ref.1, s32[16]{0:T(128)} %ds_ref.1), custom_call_target="tpu_custom_call" | custom-call | tf_op jit(solution)/shard_map/pallas_call | solution.py:457
  47.6 0.0 copy-start
  47.6 1.8 %copy.8 = bf16[768,256]{1,0:T(8,128)(2,1)} copy(bf16[768,256]{1,0:T(8,128)(2,1)} %get-tuple-element.4) | data formatting | bytes 786432
  49.4 0.0 copy-done
  49.4 0.7 %copy.9 = bf16[768,256]{1,0:T(8,128)(2,1)} copy(bf16[768,256]{1,0:T(8,128)(2,1)S(1)} %copy-done) | data formatting | bytes 786432
Async XLA Ops:
  47.6 1.8 %copy-start = (bf16[768,256]{1,0:T(8,128)(2,1)S(1)}, bf16[768,256]{1,0:T(8,128)(2,1)}, u32[]{:S(2)}) copy-start(bf16[768,256]{1,0:T(8,128)(2,1)} %get-tuple-element.5) | copy-start | bytes 1179652

commit v2 on v1

--- a/solution.py
+++ b/solution.py
@@ -10,8 +10,9 @@
 
 HOPS = 3
 NEG = -1e30
+KEY_TILES = 4
 SUB = 2
-KEY_TILES = 4
+FIRST, SECOND = range(3), range(3, 4)
 MESH = pl.DeviceIdType.MESH
 
 
@@ -34,9 +35,8 @@
     tok, width = q_ref.shape
     hd = kv_ref.shape[1] // 2
     heads = width // hd
-    half = tok // 2
-    piece = half // SUB
     kt_rows = tok // KEY_TILES
+    piece = kt_rows // SUB
     qt = math.gcd(tok, 256)
     scale = hd ** -0.5
     to_log2 = scale * math.log2(math.e)
@@ -69,8 +69,10 @@
     def rows_of(c):
         return pl.ds(c * piece, piece)
 
-    FIRST, SECOND = range(SUB), range(SUB, 2 * SUB)
-    ALL = range(2 * SUB)
+    def pieces(kts):
+        return [kt * SUB + i for kt in kts for i in range(SUB)]
+
+    ALL = range(KEY_TILES)
 
     def fwd(slot, src, device, t, c):
         return pltpu.make_async_remote_copy(
@@ -87,17 +89,17 @@
 
     @pl.when(is_even)
     def _():
-        for c in list(SECOND) + list(FIRST):
+        for c in pieces(SECOND) + pieces(FIRST):
             fwd(0, kv_ref, me + 1, 1, c).start()
 
         @pl.when(has_next)
         def _():
-            for c in FIRST:
+            for c in pieces(FIRST):
                 fwd(1, kv_ref, me + 2, 2, c).start()
 
     @pl.when(is_odd & has_next)
     def _():
-        for c in ALL:
+        for c in pieces(ALL):
             fwd(1, kv_ref, me + 2, 2, c).start()
 
     position = me * tok + lax.broadcasted_iota(jnp.int32, (1, tok), 1)
@@ -146,100 +148,80 @@
             total[stat : stat + 1, flat] = jnp.sum(e, axis=0, keepdims=True)
             weighted[stat : stat + 1, flat] = jnp.sum(e * gp, axis=0, keepdims=True)
 
-    per_half = KEY_TILES // 2
-
-    def absorb_half(t, which):
-        def run():
-            for kt in range(which * per_half, (which + 1) * per_half):
-                absorb(t, kt)
-
-        if t == 0:
-            run()
-        else:
-            when(me >= t, run)
-
-    absorb_half(0, 0)
-    absorb_half(0, 1)
-
-    @pl.when(is_even & (me >= 2))
-    def _():
-        for c in FIRST:
-            arrived(2, c)
-            fwd(3, got.at[1], me + 1, 3, c).start()
-
-    @pl.when(is_odd)
-    def _():
-        for i in range(SUB):
-            arrived(1, SECOND[i])
-
-            @pl.when(has_next)
-            def _():
-                fwd(2, got.at[0], me + 2, 3, SECOND[i]).start()
-
-            @pl.when(me >= 2)
-            def _():
-                arrived(2, FIRST[i])
-                fwd(3, got.at[1], me - 1, 1, FIRST[i]).start()
-
-    absorb_half(2, 0)
-
-    @pl.when(is_odd)
-    def _():
-        @pl.when(me >= 2)
-        def _():
-            for c in SECOND:
-                arrived(2, c)
-                fwd(3, got.at[1], me - 1, 1, c).start()
-
-        for c in FIRST:
-            arrived(1, c)
-
-    def relay_first(chunks):
+    def relay(t, kt, slot=None, device=None, to=None, cond=None):
+        for c in pieces([kt]):
+            arrived(t, c)
+            if slot is not None:
+                send = fwd(slot, got.at[t - 1], device, to, c).start
+                if cond is None:
+                    send()
+                else:
+                    when(cond, send)
+
+    def even_step(*kts):
         @pl.when(is_even & (me >= 2))
         def _():
-            for c in chunks:
-                arrived(1, c)
-
-                @pl.when(has_next)
-                def _():
-                    fwd(2, got.at[0], me + 2, 3, c).start()
-
-    relay_first(FIRST)
-    absorb_half(1, 0)
-    relay_first(SECOND)
-    absorb_half(1, 1)
-
-    @pl.when(is_odd & (me >= 3))
-    def _():
-        for c in SECOND:
-            arrived(3, c)
-            fwd(4, got.at[2], me - 1, 2, c).start()
-
-    @pl.when(me >= 3)
-    def _():
-        for c in FIRST:
-            arrived(3, c)
-
-    @pl.when(is_odd & (me >= 3))
-    def _():
-        absorb_half(2, 1)
-
-    @pl.when(me >= 3)
-    def _():
-        absorb_half(3, 0)
-
-    @pl.when(is_even & (me >= 2))
-    def _():
-        for c in SECOND:
-            arrived(2, c)
-        absorb_half(2, 1)
-
-    @pl.when(is_even & (me >= 3))
-    def _():
-        for c in SECOND:
-            arrived(3, c)
-
-    absorb_half(3, 1)
+            for t, kt in kts:
+                if t == 1:
+                    relay(1, kt, 2, me + 2, 3, has_next)
+                elif t == 2 and kt in FIRST:
+                    relay(2, kt, 3, me + 1, 3)
+                elif t == 2:
+                    relay(2, kt)
+                else:
+                    when(me >= 3, functools.partial(relay, 3, kt))
+
+    def odd_step(*kts):
+        @pl.when(is_odd)
+        def _():
+            for t, kt in kts:
+                if t == 1 and kt in SECOND:
+                    relay(1, kt, 2, me + 2, 3, has_next)
+                elif t == 1:
+                    relay(1, kt)
+                elif t == 2:
+                    when(me >= 2, functools.partial(relay, 2, kt, 3, me - 1, 1))
+                elif kt in SECOND:
+                    when(me >= 2, functools.partial(relay, 3, kt, 4, me - 1, 2))
+                else:
+                    when(me >= 2, functools.partial(relay, 3, kt))
+
+    def take(t, kt):
+        when(me >= t, functools.partial(absorb, t, kt))
+
+    for kt in range(KEY_TILES):
+        absorb(0, kt)
+    even_step((2, 0))
+    odd_step((1, 3), (2, 0))
+    take(2, 0)
+    even_step((2, 1))
+    odd_step((2, 1))
+    take(2, 1)
+    even_step((1, 0), (2, 2))
+    odd_step((2, 2), (1, 0))
+    take(1, 0)
+    odd_step((2, 3))
+    take(2, 2)
+    even_step((1, 1))
+    odd_step((1, 1))
+    take(1, 1)
+    even_step((1, 2))
+    odd_step((1, 2))
+    take(1, 2)
+    even_step((1, 3), (3, 0))
+    odd_step((3, 3), (3, 0))
+    take(1, 3)
+    take(3, 0)
+    even_step((3, 1))
+    odd_step((3, 1))
+    take(3, 1)
+    even_step((2, 3))
+    take(2, 3)
+    even_step((3, 2))
+    odd_step((3, 2))
+    take(3, 2)
+    even_step((3, 3))
+    take(3, 3)
 
     best = jnp.max(top[...], axis=0, keepdims=True)
     grow = jnp.exp2(top[...] - best)
@@ -277,16 +259,6 @@
             share[t - 1, rows, :hd] = dk.astype(jnp.bfloat16)
             share[t - 1, rows, hd:] = dv.astype(jnp.bfloat16)
 
-    def gradients_half(t, which):
-        def run():
-            for kt in range(which * per_half, (which + 1) * per_half):
-                gradients(t, kt)
-
-        if t == 0:
-            run()
-        else:
-            when(me >= t, run)
-
     def bwd(t, device, slot, c):
         return pltpu.make_async_remote_copy(
             src_ref=share.at[t - 1, rows_of(c)], dst_ref=back.at[slot, rows_of(c)],
@@ -303,85 +275,85 @@
         both = share[t - 1, rows, :].astype(jnp.float32) + back[t - 1, rows, :].astype(jnp.float32)
         share[t - 1, rows, :] = both.astype(jnp.bfloat16)
 
-    gradients_half(3, 0)
-
-    @pl.when(me >= 3)
-    def _():
-        @pl.when(is_even)
-        def _():
-            for c in FIRST:
-                bwd(3, me - 2, 0, c).start()
-
+    def give(t, kt):
+        when(me >= t, functools.partial(gradients, t, kt))
+
+    def send_back(t, kt, device, slot, merged=None):
+        for c in pieces([kt]):
+            if merged is True:
+                merge(t, c)
+            elif merged is not None:
+                when(merged, functools.partial(merge, t, c))
+            bwd(t, device, slot, c).start()
+
+    def even_back(*kts):
+        @pl.when(is_even & (me >= 2))
+        def _():
+            for t, kt in kts:
+                if t == 1:
+                    send_back(1, kt, me + 1, 1, has_next)
+                elif t == 2 and kt in FIRST:
+                    send_back(2, kt, me - 2, 4, True)
+                elif t == 2:
+                    send_back(2, kt, me + 1, 2)
+                else:
+                    when(me >= 3, functools.partial(send_back, 3, kt, me - 2, 0))
+
+    def odd_back(*kts):
         @pl.when(is_odd)
         def _():
-            for c in FIRST:
-                bwd(3, me - 1, 1, c).start()
-
-    gradients_half(2, 1)
-
-    @pl.when(is_even & (me >= 2))
-    def _():
-        for c in SECOND:
-            bwd(2, me + 1, 2, c).start()
-
-    gradients_half(3, 1)
-
-    @pl.when(me >= 3)
-    def _():
-        @pl.when(is_even)
-        def _():
-            for c in SECOND:
-                bwd(3, me - 2, 0, c).start()
-
-        @pl.when(is_odd)
-        def _():
-            for c in SECOND:
-                merge(3, c)
-                bwd(3, me - 2, 0, c).start()
-
-    gradients_half(2, 0)
-
-    @pl.when(is_even & (me >= 2))
-    def _():
-        for c in FIRST:
-            merge(2, c)
-            bwd(2, me - 2, 4, c).start()
-
-    def send_one(chunks, add_odd):
-        @pl.when(is_even & (me >= 2))
-        def _():
-            for c in chunks:
-                @pl.when(has_next)
-                def _():
-                    merge(1, c)
-
-                bwd(1, me + 1, 1, c).start()
-
-        @pl.when(is_odd)
-        def _():
-            for c in chunks:
-                if add_odd:
-                    @pl.when(has_next)
-                    def _():
-                        merge(1, c)
-
-                bwd(1, me - 1, 3, c).start()
-
-    gradients_half(1, 0)
-    send_one(FIRST, False)
-    gradients_half(1, 1)
-    send_one(SECOND, True)
-    gradients_half(0, 0)
-    gradients_half(0, 1)
-
-    @pl.when(is_odd & (me >= 2))
-    def _():
-        for c in ALL:
-            merge(2, c)
-            bwd(2, me - 2, 4, c).start()
+            for t, kt in kts:
+                if t == 1:
+                    send_back(1, kt, me - 1, 3, has_next if kt in SECOND else None)
+                elif t == 2:
+                    when(me >= 2, functools.partial(send_back, 2, kt, me - 2, 4, True))
+                elif kt in FIRST:
+                    when(me >= 2, functools.partial(send_back, 3, kt, me - 1, 1))
+                else:
+                    when(me >= 2, functools.partial(send_back, 3, kt, me - 2, 0, True))
+
+    give(3, 0)
+    even_back((3, 0))
+    odd_back((3, 0))
+    give(2, 3)
+    even_back((2, 3))
+    give(3, 1)
+    even_back((3, 1))
+    odd_back((3, 1))
+    give(3, 2)
+    even_back((3, 2))
+    odd_back((3, 2))
+    give(3, 3)
+    even_back((3, 3))
+    give(1, 0)
+    odd_back((1, 0))
+    give(1, 1)
+    odd_back((1, 1), (3, 3))
+    even_back((1, 0))
+    give(1, 2)
+    odd_back((1, 2))
+    give(2, 0)
+    even_back((2, 0), (1, 1))
+    give(2, 1)
+    even_back((2, 1))
+    give(2, 2)
+    even_back((2, 2))
+    give(1, 3)
+    gradients(0, 0)
+    even_back((1, 2))
+    odd_back((2, 0))
+    gradients(0, 1)
+    odd_back((1, 3))
+    gradients(0, 2)
+    even_back((1, 3))
+    odd_back((2, 1))
+    gradients(0, 3)
+    odd_back((2, 2))
 
     for h in range(heads):
         dq_ref[:, h * hd : (h + 1) * hd] = dq_t[:, h * tok : (h + 1) * tok].T.astype(jnp.bfloat16)
+
+    odd_back((2, 3))
 
     def add_back(slot, c):
         returned(slot, c)
@@ -390,27 +362,27 @@
 
     @pl.when(is_even)
     def _():
-        for c in ALL:
+        for c in pieces(ALL):
             add_back(3, c)
 
         @pl.when(has_next)
         def _():
-            for c in FIRST:
+            for c in pieces(FIRST):
                 add_back(4, c)
 
     @pl.when(is_odd & has_next)
     def _():
-        for c in ALL:
+        for c in pieces(ALL):
             add_back(4, c)
 
     dkv_ref[...] = own[...].astype(jnp.bfloat16)
 
     def sent(slot, chunks):
-        for c in chunks:
+        for c in pieces(chunks):
             fwd(slot, kv_ref, pair, 1, c).wait_send()
 
     def sent_back(t, chunks):
-        for c in chunks:
+        for c in pieces(chunks):
             bwd(t, pair, 0, c).wait_send()
 
     @pl.when(is_even)
@@ -453,7 +425,7 @@
     stats = blocks * KEY_TILES
     bf16, f32 = jnp.bfloat16, jnp.float32
     vmem = pl.BlockSpec(memory_space=pltpu.VMEM)
-    pieces = 2 * SUB
+    pieces = KEY_TILES * SUB
     return pl.pallas_call(
         functools.partial(kernel, n),
         out_shape=(
@@ -484,7 +456,7 @@
             pltpu.SemaphoreType.DMA((5, pieces)),
         ],
         compiler_params=pltpu.CompilerParams(
-            collective_id=0, has_side_effects=True, vmem_limit_bytes=63 * 2**20
+            collective_id=0, has_side_effects=True, vmem_limit_bytes=56 * 2**20
         ),
     )(query, d_out, key_value, doc_starts)
 

time: 50.4 us -> 46 us (0.913)
  Pallas kernels: 46.9 us -> 42.6 us
    pallas_call x1, Pallas kernels: 46.9 us -> 42.6 us  [shards(): pl.pallas_call(functools.partial(kernel, n), out_shape=(jax.ShapeDtypeStr...]
where the time goes in v2:
time: 46 us; the launch traced here: 45.8 us
  Pallas kernels  42.6 us (93%)
  local copies, waits for them, and re-layouts  2.57 us (6%)
  between operations  0.65 us (1%)
    pallas_call x1, Pallas kernels, shards(): pl.pallas_call(functools.partial(kernel, n), out_shape=(jax.ShapeDtypeStr...  42.6 us
    unnamed x4, local copies, waits for them, and re-layouts  2.57 us

profile of v2, /device:TPU:10, one launch (start us, length us, event | category | flops | bytes accessed | tf_op | source)
XLA Modules:
  0.0 45.8 jit_solution(8222406266642268012)
XLA Ops:
  0.6 42.6 %shard_map.59 = (bf16[768,256]{1,0:T(8,128)(2,1)}, bf16[768,256]{1,0:T(8,128)(2,1)}) custom-call(bf16[768,256]{1,0:T(8,128)(2,1)} %q_ref.1, bf16[768,256]{1,0:T(8,128)(2,1)} %g_ref.1, bf16[768,256]{1,0:T(8,128)(2,1)} %kv_ref.1, s32[16]{0:T(128)} %ds_ref.1), custom_call_target="tpu_custom_call" | custom-call | tf_op jit(solution)/shard_map/pallas_call | solution.py:429
  43.2 0.0 copy-start
  43.2 1.8 %copy.8 = bf16[768,256]{1,0:T(8,128)(2,1)} copy(bf16[768,256]{1,0:T(8,128)(2,1)} %get-tuple-element.4) | data formatting | bytes 786432
  45.1 0.0 copy-done
  45.1 0.7 %copy.9 = bf16[768,256]{1,0:T(8,128)(2,1)} copy(bf16[768,256]{1,0:T(8,128)(2,1)S(1)} %copy-done) | data formatting | bytes 786432
Async XLA Ops:
  43.2 1.8 %copy-start = (bf16[768,256]{1,0:T(8,128)(2,1)S(1)}, bf16[768,256]{1,0:T(8,128)(2,1)}, u32[]{:S(2)}) copy-start(bf16[768,256]{1,0:T(8,128)(2,1)} %get-tuple-element.5) | copy-start | bytes 1179652

commit v3 on v2

--- a/solution.py
+++ b/solution.py
@@ -25,7 +25,8 @@
 
 
 def kernel(
-    n, q_ref, g_ref, kv_ref, ds_ref, dq_ref, dkv_ref,
+    n, q_in, g_in, kv_in, ds_ref, dq_out, dkv_ref,
+    q_ref, g_ref, kv_ref, dq_ref, io_sem,
     got, expo, gprob, top, total, weighted, factor, delta, low_p, low_g, dq_t, own, share, back,
     own_rows, f_send, f_recv, b_send, b_recv,
 ):
@@ -42,6 +43,13 @@
     to_log2 = scale * math.log2(math.e)
     has_next = me + 2 < n
 
+    load_kv = pltpu.make_async_copy(kv_in, kv_ref, io_sem.at[0])
+    load_q = pltpu.make_async_copy(q_in, q_ref, io_sem.at[1])
+    load_g = pltpu.make_async_copy(g_in, g_ref, io_sem.at[2])
+    store_dq = pltpu.make_async_copy(dq_ref, dq_out, io_sem.at[3])
+    for load in (load_kv, load_q, load_g):
+        load.start()
+
     barrier = pltpu.get_barrier_semaphore()
     pair = me + 1 - 2 * odd
 
@@ -57,50 +65,6 @@
     @pl.when(me >= 2)
     def _():
         greet(me - 2)
-
-    @pl.when(has_next & (me >= 2))
-    def _():
-        pl.semaphore_wait(barrier, 3)
-
-    @pl.when(jnp.logical_not(has_next & (me >= 2)))
-    def _():
-        pl.semaphore_wait(barrier, 2)
-
-    def rows_of(c):
-        return pl.ds(c * piece, piece)
-
-    def pieces(kts):
-        return [kt * SUB + i for kt in kts for i in range(SUB)]
-
-    ALL = range(KEY_TILES)
-
-    def fwd(slot, src, device, t, c):
-        return pltpu.make_async_remote_copy(
-            src_ref=src.at[rows_of(c)], dst_ref=got.at[t - 1, rows_of(c)],
-            send_sem=f_send.at[slot, c], recv_sem=f_recv.at[t - 1, c],
-            device_id={"ctx": device}, device_id_type=MESH,
-        )
-
-    def arrived(t, c):
-        fwd(0, kv_ref, pair, t, c).wait_recv()
-
-    def when(cond, f):
-        pl.when(cond)(f)
-
-    @pl.when(is_even)
-    def _():
-        for c in pieces(SECOND) + pieces(FIRST):
-            fwd(0, kv_ref, me + 1, 1, c).start()
-
-        @pl.when(has_next)
-        def _():
-            for c in pieces(FIRST):
-                fwd(1, kv_ref, me + 2, 2, c).start()
-
-    @pl.when(is_odd & has_next)
-    def _():
-        for c in pieces(ALL):
-            fwd(1, kv_ref, me + 2, 2, c).start()
 
     position = me * tok + lax.broadcasted_iota(jnp.int32, (1, tok), 1)
     owners = jnp.zeros((1, tok), jnp.int32)
@@ -112,6 +76,55 @@
     total[...] = jnp.zeros_like(total)
     weighted[...] = jnp.zeros_like(weighted)
     dq_t[...] = jnp.zeros_like(dq_t)
+
+    @pl.when(has_next & (me >= 2))
+    def _():
+        pl.semaphore_wait(barrier, 3)
+
+    @pl.when(jnp.logical_not(has_next & (me >= 2)))
+    def _():
+        pl.semaphore_wait(barrier, 2)
+
+    def rows_of(c):
+        return pl.ds(c * piece, piece)
+
+    load_kv.wait()
+
+    def pieces(kts):
+        return [kt * SUB + i for kt in kts for i in range(SUB)]
+
+    ALL = range(KEY_TILES)
+
+    def fwd(slot, src, device, t, c):
+        return pltpu.make_async_remote_copy(
+            src_ref=src.at[rows_of(c)], dst_ref=got.at[t - 1, rows_of(c)],
+            send_sem=f_send.at[slot, c], recv_sem=f_recv.at[t - 1, c],
+            device_id={"ctx": device}, device_id_type=MESH,
+        )
+
+    def arrived(t, c):
+        fwd(0, kv_ref, pair, t, c).wait_recv()
+
+    def when(cond, f):
+        pl.when(cond)(f)
+
+    @pl.when(is_even)
+    def _():
+        for c in pieces(SECOND) + pieces(FIRST):
+            fwd(0, kv_ref, me + 1, 1, c).start()
+
+        @pl.when(has_next)
+        def _():
+            for c in pieces(FIRST):
+                fwd(1, kv_ref, me + 2, 2, c).start()
+
+    @pl.when(is_odd & has_next)
+    def _():
+        for c in pieces(ALL):
+            fwd(1, kv_ref, me + 2, 2, c).start()
+
+    load_q.wait()
+    load_g.wait()
 
     def tiles():
         for h in range(heads):
@@ -353,6 +366,7 @@
     for h in range(heads):
         dq_ref[:, h * hd : (h + 1) * hd] = dq_t[:, h * tok : (h + 1) * tok].T.astype(jnp.bfloat16)
 
+    store_dq.start()
     odd_back((2, 3))
 
     def add_back(slot, c):
@@ -376,6 +390,7 @@
             add_back(4, c)
 
     dkv_ref[...] = own[...].astype(jnp.bfloat16)
+    store_dq.wait()
 
     def sent(slot, chunks):
         for c in pieces(chunks):
@@ -425,6 +440,7 @@
     stats = blocks * KEY_TILES
     bf16, f32 = jnp.bfloat16, jnp.float32
     vmem = pl.BlockSpec(memory_space=pltpu.VMEM)
+    hbm = pl.BlockSpec(memory_space=pl.ANY)
     pieces = KEY_TILES * SUB
     return pl.pallas_call(
         functools.partial(kernel, n),
@@ -432,9 +448,14 @@
             jax.ShapeDtypeStruct(query.shape, bf16),
             jax.ShapeDtypeStruct(key_value.shape, bf16),
         ),
-        in_specs=[vmem, vmem, vmem, pl.BlockSpec(memory_space=pltpu.SMEM)],
-        out_specs=(vmem, vmem),
+        in_specs=[hbm, hbm, hbm, pl.BlockSpec(memory_space=pltpu.SMEM)],
+        out_specs=(hbm, vmem),
         scratch_shapes=[
+            pltpu.VMEM(query.shape, bf16),
+            pltpu.VMEM(d_out.shape, bf16),
+            pltpu.VMEM(key_value.shape, bf16),
+            pltpu.VMEM(query.shape, bf16),
+            pltpu.SemaphoreType.DMA((4,)),
             pltpu.VMEM((HOPS, tok, 2 * hd), bf16),
             pltpu.VMEM((blocks, tok, flat), f32),
             pltpu.VMEM((blocks, tok, flat), f32),

time: 46 us -> 45.2 us (0.983)
  Pallas kernels: 42.6 us -> 41.9 us
    pallas_call x1, Pallas kernels: 42.6 us -> 41.9 us  [shards(): pl.pallas_call(functools.partial(kernel, n), out_shape=(jax.ShapeDtypeStr...]
where the time goes in v3:
time: 45.2 us; the launch traced here: 45.1 us
  Pallas kernels  41.9 us (93%)
  local copies, waits for them, and re-layouts  2.57 us (6%)
  between operations  0.65 us (1%)
    pallas_call x1, Pallas kernels, shards(): pl.pallas_call(functools.partial(kernel, n), out_shape=(jax.ShapeDtypeStr...  41.9 us
    unnamed x4, local copies, waits for them, and re-layouts  2.57 us

profile of v3, /device:TPU:10, one launch (start us, length us, event | category | flops | bytes accessed | tf_op | source)
XLA Modules:
  0.0 45.1 jit_solution(1000123764513731548)
XLA Ops:
  0.6 41.9 %shard_map.59 = (bf16[768,256]{1,0:T(8,128)(2,1)}, bf16[768,256]{1,0:T(8,128)(2,1)}) custom-call(bf16[768,256]{1,0:T(8,128)(2,1)} %q_in.1, bf16[768,256]{1,0:T(8,128)(2,1)} %g_in.1, bf16[768,256]{1,0:T(8,128)(2,1)} %kv_in.1, s32[16]{0:T(128)} %ds_ref.1), custom_call_target="tpu_custom_call" | custom-call | tf_op jit(solution)/shard_map/pallas_call | solution.py:445
  42.5 0.0 copy-start
  42.5 1.8 %copy.8 = bf16[768,256]{1,0:T(8,128)(2,1)} copy(bf16[768,256]{1,0:T(8,128)(2,1)} %get-tuple-element.4) | data formatting | bytes 786432
  44.3 0.0 copy-done
  44.3 0.7 %copy.9 = bf16[768,256]{1,0:T(8,128)(2,1)} copy(bf16[768,256]{1,0:T(8,128)(2,1)S(1)} %copy-done) | data formatting | bytes 786432
Async XLA Ops:
  42.5 1.8 %copy-start = (bf16[768,256]{1,0:T(8,128)(2,1)S(1)}, bf16[768,256]{1,0:T(8,128)(2,1)}, u32[]{:S(2)}) copy-start(bf16[768,256]{1,0:T(8,128)(2,1)} %get-tuple-element.5) | copy-start | bytes 1179652
